TPU v7x, 32 devices: a whole 2x2x4 slice. The times are simulated.
32 devices in a mesh: dp: 8 (over z, y), rep: 4 (over x, core).
Axes of the slice: x: 2, y: 2, z: 4, core: 2. Of those that a mesh axis runs over, the one named last changes fastest.
Arguments:
- enc: bfloat16 [64, 48, 640], P(('dp', 'rep')), may hold values from -6 to 6
- pred: bfloat16 [64, 17, 640], P(('dp', 'rep')), may hold values from -6 to 6
- labels: int32 [64, 16], P(('dp', 'rep')), may hold values from 1 to 4095
- frame_len: int32 [64], P(('dp', 'rep')), may hold values from 24 to 48, as said below
- label_len: int32 [64], P(('dp', 'rep')), may hold values from 1 to 16, as said below
- w_enc: bfloat16 [640, 640], replicated, may hold values from -0.25 to 0.25
- w_pred: bfloat16 [640, 640], replicated, may hold values from -0.25 to 0.25
- b_joint: bfloat16 [640], replicated, may hold values from -3 to 3
- w_out: bfloat16 [640, 4096], replicated, may hold values from -0.69921875 to 0.69921875
- b_out: bfloat16 [4096], replicated, may hold values from -5 to 5
Outputs:
- step_enc: float32 [640, 640], replicated
- step_pred: float32 [640, 640], replicated
- step_out: float32 [640, 4096], replicated
- step_bias_out: float32 [4096], replicated
- step_bias_joint: float32 [640], replicated
- mean_loss: float32 [], replicated
Inputs may be any that keep to these rules, and one draw needn't show every extreme that they name: `frame_len`: the last utterance has all 48 frames. `label_len`: the last utterance has all 16 labels.
All inputs are finite; a program needn't handle non-finite values.
Results may differ from a plain program's by a relative error of at most 0.0055.
Values sent between devices are 32-bit elements; how exact they have to be, the bound alone decides.
No kernel may reach another device: no remote copies, remote signals or barrier semaphores. Data moves between devices by JAX's collectives and lax.ppermute only.
A program may use at most 256 MiB of HBM per device.

v0:
```python
import jax
import jax.numpy as jnp
from jax import lax
from jax.sharding import PartitionSpec as P

NEG = -1e30
EPS = 1e-06


def diagonal_index(num_frames, count_labels):
    diagonals = jnp.arange(num_frames + count_labels - 1, dtype=jnp.int32)
    positions = jnp.arange(count_labels, dtype=jnp.int32)
    return diagonals[:, None] - positions[None, :]


def skewed(grid):
    utterances, num_frames, count_labels = grid.shape
    positions = jnp.arange(count_labels, dtype=jnp.int32)
    frame_index = diagonal_index(num_frames, count_labels)
    inside = (frame_index >= 0) & (frame_index < num_frames)
    picked = grid[:, jnp.clip(frame_index, 0, num_frames - 1), positions[None, :]]
    picked = jnp.where(inside[None, :, :], picked, NEG)
    return jnp.transpose(picked, (1, 0, 2))


def unskewed(diag_grid, num_frames):
    count_labels = diag_grid.shape[2]
    by_utterance = jnp.transpose(diag_grid, (1, 0, 2))
    frame_ids = jnp.arange(num_frames, dtype=jnp.int32)
    positions = jnp.arange(count_labels, dtype=jnp.int32)
    return by_utterance[:, frame_ids[:, None] + positions[None, :], positions[None, :]]


def lattice(blank, emit, frame_len, label_len):
    utterances, num_frames, count_labels = blank.shape
    positions = jnp.arange(count_labels, dtype=jnp.int32)
    frame_index = diagonal_index(num_frames, count_labels)
    blank_diag = skewed(blank)
    emit_diag = skewed(emit)
    neg_block = jnp.full((1, utterances, count_labels), NEG, jnp.float32)
    neg_col = jnp.full((utterances, 1), NEG, jnp.float32)
    neg_grid = jnp.full((utterances, count_labels), NEG, jnp.float32)
    frame_count = frame_len[:, None]
    label_count = label_len[:, None]
    terminal = jnp.where(positions[None, :] == label_count, 0.0, NEG).astype(jnp.float32)
    first_diag = jnp.broadcast_to(
        jnp.where(positions == 0, 0.0, NEG).astype(jnp.float32)[None, :], (utterances, count_labels)
    )
    blank_prev = jnp.concatenate([neg_block, blank_diag[:-1]], axis=0)
    emit_prev = jnp.concatenate([neg_block, emit_diag[:-1]], axis=0)
    steps_total = frame_index.shape[0]
    step_ids = jnp.arange(steps_total, dtype=jnp.int32)

    def both_ways(carry, inputs):
        alpha_prev, beta_next = carry
        step_id, blank_fwd, emit_fwd, frames_fwd, blank_back, emit_back, frames_back = inputs
        top_term = alpha_prev + blank_fwd
        left_term = jnp.concatenate([neg_col, (alpha_prev + emit_fwd)[:, :-1]], axis=1)
        alpha_cell = jnp.logaddexp(top_term, left_term)
        inside = (frames_fwd >= 0) & (frames_fwd < num_frames)
        alpha_cell = jnp.where(inside[None, :], alpha_cell, NEG)
        alpha_cell = jnp.where(step_id == 0, first_diag, alpha_cell)
        frames_row = frames_back[None, :]
        below = jnp.where(
            frames_row == frame_count - 1,
            terminal,
            jnp.where(frames_row >= frame_count, neg_grid, beta_next),
        )
        right_term = jnp.concatenate([beta_next[:, 1:], neg_col], axis=1)
        beta_cell = jnp.logaddexp(below + blank_back, right_term + emit_back)
        live = (positions[None, :] <= label_count) & (frames_row < frame_count) & (frames_row >= 0)
        beta_cell = jnp.where(live, beta_cell, NEG)
        return ((alpha_cell, beta_cell), (alpha_cell, beta_cell, below))

    inputs = (
        step_ids,
        blank_prev,
        emit_prev,
        frame_index,
        jnp.flip(blank_diag, 0),
        jnp.flip(emit_diag, 0),
        jnp.flip(frame_index, 0),
    )
    unused_last, (alpha_diag, beta_rev, below_rev) = lax.scan(
        both_ways, (first_diag, neg_grid), inputs
    )
    alpha = unskewed(alpha_diag, num_frames)
    beta = unskewed(jnp.flip(beta_rev, 0), num_frames)
    below = unskewed(jnp.flip(below_rev, 0), num_frames)
    return (alpha, beta, below)


def joint_forward(enc_row, pred_row, label_row, w_enc, w_pred, b_joint, w_out, b_out):
    num_frames = enc_row.shape[0]
    count_labels = pred_row.shape[0]
    joint_width = w_enc.shape[1]
    vocab_size = w_out.shape[1]
    enc_proj = jnp.dot(enc_row, w_enc, preferred_element_type=jnp.float32)
    pred_proj = jnp.dot(pred_row, w_pred, preferred_element_type=jnp.float32) + b_joint.astype(
        jnp.float32
    )
    hidden = jnp.tanh(enc_proj[:, None, :] + pred_proj[None, :, :]).astype(jnp.bfloat16)
    hidden = lax.optimization_barrier(hidden.reshape(num_frames * count_labels, joint_width))
    logits = jnp.dot(hidden, w_out, preferred_element_type=jnp.float32) + b_out.astype(jnp.float32)
    log_probs = jax.nn.log_softmax(logits, axis=-1)
    targets = jnp.concatenate([label_row, jnp.ones((1,), jnp.int32)])
    target_cols = jnp.tile(targets, num_frames)
    vocab_pos = jnp.arange(vocab_size, dtype=jnp.int32)
    is_target = vocab_pos[None, :] == target_cols[:, None]
    emit = jnp.sum(jnp.where(is_target, log_probs, 0.0), axis=1).reshape(num_frames, count_labels)
    blank = log_probs[:, 0].reshape(num_frames, count_labels)
    return (hidden, log_probs, blank, emit)


def joint_backward(
    enc_row, pred_row, label_row, hidden, log_probs, blank, emit, alpha, beta, below, w_out
):
    num_frames = enc_row.shape[0]
    count_labels = pred_row.shape[0]
    joint_width = hidden.shape[1]
    vocab_size = w_out.shape[1]
    targets = jnp.concatenate([label_row, jnp.ones((1,), jnp.int32)])
    target_cols = jnp.tile(targets, num_frames)
    vocab_pos = jnp.arange(vocab_size, dtype=jnp.int32)
    is_target = vocab_pos[None, :] == target_cols[:, None]
    log_total = beta[0, 0]
    right = jnp.concatenate([beta[:, 1:], jnp.full((num_frames, 1), NEG, jnp.float32)], axis=1)
    blank_occ = jnp.exp(alpha + blank + below - log_total).reshape(-1)
    emit_occ = jnp.exp(alpha + emit + right - log_total).reshape(-1)
    probs = jnp.exp(log_probs)
    grad_logits = probs * (blank_occ + emit_occ)[:, None]
    grad_logits = grad_logits - jnp.where(vocab_pos[None, :] == 0, blank_occ[:, None], 0.0)
    grad_logits = grad_logits - jnp.where(is_target, emit_occ[:, None], 0.0)
    grad_logits = lax.optimization_barrier(grad_logits.astype(jnp.bfloat16))
    grad_out = lax.dot_general(
        hidden, grad_logits, (((0,), (0,)), ((), ())), preferred_element_type=jnp.float32
    )
    grad_bias_out = jnp.sum(grad_logits.astype(jnp.float32), axis=0)
    grad_hidden = lax.dot_general(
        grad_logits, w_out, (((1,), (1,)), ((), ())), preferred_element_type=jnp.float32
    )
    hidden_wide = hidden.astype(jnp.float32)
    grad_pre = (grad_hidden * (1.0 - hidden_wide * hidden_wide)).reshape(
        num_frames, count_labels, joint_width
    )
    grad_enc_proj = lax.optimization_barrier(jnp.sum(grad_pre, axis=1).astype(jnp.bfloat16))
    grad_pred_proj = lax.optimization_barrier(jnp.sum(grad_pre, axis=0).astype(jnp.bfloat16))
    grad_enc = lax.dot_general(
        enc_row, grad_enc_proj, (((0,), (0,)), ((), ())), preferred_element_type=jnp.float32
    )
    grad_pred = lax.dot_general(
        pred_row, grad_pred_proj, (((0,), (0,)), ((), ())), preferred_element_type=jnp.float32
    )
    grad_bias_joint = jnp.sum(grad_pred_proj.astype(jnp.float32), axis=0)
    return (-log_total, (grad_enc, grad_pred, grad_out, grad_bias_out, grad_bias_joint))


def local_sums(enc, pred, labels, frame_len, label_len, w_enc, w_pred, b_joint, w_out, b_out):

    def forward_one(unused_carry, inputs):
        enc_row, pred_row, label_row = inputs
        return (
            None,
            joint_forward(enc_row, pred_row, label_row, w_enc, w_pred, b_joint, w_out, b_out),
        )

    unused_none, (hidden, log_probs, blank, emit) = lax.scan(forward_one, None, (enc, pred, labels))
    alpha, beta, below = lattice(blank, emit, frame_len, label_len)
    initial = (
        jnp.zeros(w_enc.shape, jnp.float32),
        jnp.zeros(w_pred.shape, jnp.float32),
        jnp.zeros(w_out.shape, jnp.float32),
        jnp.zeros(b_out.shape, jnp.float32),
        jnp.zeros(b_joint.shape, jnp.float32),
    )

    def backward_one(carry, inputs):
        loss_sum, grad_sums = carry
        loss_one, grads_one = joint_backward(*inputs, w_out)
        added = tuple((total + term for total, term in zip(grad_sums, grads_one)))
        return ((loss_sum + loss_one, added), None)

    (loss_sum, grads), unused_ys = lax.scan(
        backward_one,
        (jnp.float32(0.0), initial),
        (enc, pred, labels, hidden, log_probs, blank, emit, alpha, beta, below),
    )
    return (loss_sum, grads)


def squares(items):
    total_sq = jnp.float32(0.0)
    for item in items:
        total_sq = total_sq + jnp.sum(item * item)
    return total_sq


def per_device(enc, pred, labels, frame_len, label_len, w_enc, w_pred, b_joint, w_out, b_out):
    loss_local, grads = local_sums(
        enc, pred, labels, frame_len, label_len, w_enc, w_pred, b_joint, w_out, b_out
    )
    count_local = jnp.sum(label_len).astype(jnp.float32)
    param_count = jnp.float32(w_enc.size + w_pred.size + w_out.size + b_out.size + b_joint.size)
    loss_total, label_total = lax.psum((loss_local, count_local), ("dp", "rep"))
    summed = lax.psum((grads[0], grads[1], grads[2], grads[3], grads[4]), ("dp", "rep"))
    scale = lax.rsqrt(squares(summed) / param_count + EPS)
    result = tuple((item * scale for item in summed))
    return (result[0], result[1], result[2], result[3], result[4], loss_total / label_total)


def solution(mesh):
    in_specs = (
        P(("dp", "rep"), None, None),
        P(("dp", "rep"), None, None),
        P(("dp", "rep"), None),
        P(("dp", "rep")),
        P(("dp", "rep")),
        P(),
        P(),
        P(),
        P(),
        P(),
    )
    out_specs = (P(), P(), P(), P(), P(), P())
    return jax.shard_map(
        per_device, mesh=mesh, in_specs=in_specs, out_specs=out_specs, check_vma=False
    )
```

profile of v0, /device:TPU:0, one launch (start us, length us, event | category | flops | bytes accessed | tf_op | source)
XLA Modules:
  0.0 639.8 jit_solution(4801691328892887368)
XLA Ops:
  11.1 88.6 %while.58 = (s32[]{:T(128)}, bf16[2,816,640]{2,1,0:T(8,128)(2,1)}, f32[2,816,4096]{2,1,0:T(8,128)}, f32[2,48,17]{2,1,0:T(8,128)S(1)}, f32[2,48,17]{2,1,0:T(8,128...) while((s32[]{:T(128)}, bf16[2,816,640]{2,1,0:T(8,128)(2,1)}, ...), condition=%wide.region_4.5_spmd, body=%wide.region_0.4_spmd.sunk | while | flops 4369261056 | bytes 147507888 | solution.py:167
  16.4 7.5 %add_reduce_fusion.2 = (f32[816]{0:T(1024)S(1)}, f32[816,4096]{1,0:T(8,128)S(1)}) fusion(f32[4096]{0:T(1024)S(1)} %convert_element_type.65, bf16[816,640]{1,0:T(8,128)(2,1)S(1)} %convert_element_type.64, bf16[640,4096]{1,0:T(8,128)(2,1)} %get-tuple-element.1143), kind=kOutput, calls=%fused_computation.66.clone.1 | convolution fusion | flops 4284873984 | bytes 19676352 | tf_op jit(solution)/shard_map/while/body/eval_jaxpr/dot_general | solution.py:104
  28.9 12.7 %select_reduce_fusion.2 = (f32[816]{0:T(1024)S(1)}, f32[816,4096]{1,0:T(8,128)}) fusion(s32[816]{0:T(1024)S(1)} %eq.178, f32[816]{0:T(1024)S(1)} %log.11, f32[816]{0:T(1024)S(1)} %get-tuple-element.1053, f32[816,4096]{1,0:T(8,128)} %copy-done.1, f32[4096]{0:T(1024)S(1)} %convert_element_type.65), kind=kLoop, calls=%fused_computation.62.clone.1 | loop fusion | flops 20053200 | bytes 26768128 | tf_op jit(solution)/shard_map/while/body/eval_jaxpr/reduce_sum | solution.py:110
  43.1 11.3 %bitcast_dynamic-update-slice_fusion.5 = f32[2,816,4096]{2,1,0:T(8,128)} fusion(f32[2,816,4096]{2,1,0:T(8,128)} %get-tuple-element.1120, s32[]{:T(128)} %get-tuple-element.1118, f32[816,4096]{1,0:T(8,128)} %get-tuple-element.1054), kind=kLoop, calls=%fused_computation.61.clone.1 | loop fusion | bytes 26739200 | tf_op jit(solution)/shard_map/while/body/jit(dynamic_update_index_in_dim)/dynamic_update_slice | solution.py:167
  60.6 7.5 %add_reduce_fusion.2 = (f32[816]{0:T(1024)S(1)}, f32[816,4096]{1,0:T(8,128)S(1)}) fusion(f32[4096]{0:T(1024)S(1)} %convert_element_type.65, bf16[816,640]{1,0:T(8,128)(2,1)S(1)} %convert_element_type.64, bf16[640,4096]{1,0:T(8,128)(2,1)} %get-tuple-element.1143), kind=kOutput, calls=%fused_computation.66.clone.1 | convolution fusion | flops 4284873984 | bytes 19676352 | tf_op jit(solution)/shard_map/while/body/eval_jaxpr/dot_general | solution.py:104
  73.2 12.7 %select_reduce_fusion.2 = (f32[816]{0:T(1024)S(1)}, f32[816,4096]{1,0:T(8,128)}) fusion(s32[816]{0:T(1024)S(1)} %eq.178, f32[816]{0:T(1024)S(1)} %log.11, f32[816]{0:T(1024)S(1)} %get-tuple-element.1053, f32[816,4096]{1,0:T(8,128)} %copy-done.1, f32[4096]{0:T(1024)S(1)} %convert_element_type.65), kind=kLoop, calls=%fused_computation.62.clone.1 | loop fusion | flops 20053200 | bytes 26768128 | tf_op jit(solution)/shard_map/while/body/eval_jaxpr/reduce_sum | solution.py:110
  87.3 11.3 %bitcast_dynamic-update-slice_fusion.5 = f32[2,816,4096]{2,1,0:T(8,128)} fusion(f32[2,816,4096]{2,1,0:T(8,128)} %get-tuple-element.1120, s32[]{:T(128)} %get-tuple-element.1118, f32[816,4096]{1,0:T(8,128)} %get-tuple-element.1054), kind=kLoop, calls=%fused_computation.61.clone.1 | loop fusion | bytes 26739200 | tf_op jit(solution)/shard_map/while/body/jit(dynamic_update_index_in_dim)/dynamic_update_slice | solution.py:167
  100.8 12.3 %gather_fusion = f32[1088,2]{1,0:T(8,128)S(1)} fusion(f32[2,48,17]{0,1,2:T(8,128)S(1)} %copy.55, s32[1088]{0:T(1024)S(1)} %reshape.180), kind=kCustom, calls=%fused_computation | custom fusion | bytes 26112 | tf_op jit(solution)/shard_map/gather | solution.py:21
  113.6 12.1 %gather_fusion.1 = f32[1088,2]{1,0:T(8,128)S(1)} fusion(f32[2,48,17]{0,1,2:T(8,128)S(1)} %copy.57, s32[1088]{0:T(1024)S(1)} %reshape.180), kind=kCustom, calls=%fused_computation.1 | custom fusion | bytes 26112 | tf_op jit(solution)/shard_map/gather | solution.py:21
  126.3 106.5 %while.59 = (s32[]{:T(128)}, f32[2,17]{1,0:T(2,128)S(1)}, f32[2,17]{1,0:T(2,128)S(1)}, f32[64,2,17]{2,1,0:T(2,128)S(1)}, f32[64,2,17]{2,1,0:T(2,128)S(1)}, /*ind...) while((s32[]{:T(128)}, f32[2,17]{1,0:T(2,128)S(1)}, ...), condition=%wide.region_6.7_spmd.clone, body=%wide.region_5.6_spmd.clone.sunk | while | flops 1434 | bytes 22799 | solution.py:84
  233.9 9.8 %gather_fusion.2 = f32[816,2]{1,0:T(8,128)S(1)} fusion(f32[2,64,17]{0,1,2:T(8,128)S(1)} %bitcast.183, s32[816]{0:T(1024)S(1)} %reshape.192), kind=kCustom, calls=%fused_computation.2 | custom fusion | bytes 19584 | tf_op jit(solution)/shard_map/gather | solution.py:31
  245.2 10.0 %gather_fusion.4 = f32[816,2]{1,0:T(8,128)S(1)} fusion(f32[2,64,17]{0,1,2:T(8,128)S(1)} %bitcast.185, s32[816]{0:T(1024)S(1)} %reshape.192), kind=kCustom, calls=%fused_computation.4 | custom fusion | bytes 19584 | tf_op jit(solution)/shard_map/gather | solution.py:31
  256.3 9.8 %gather_fusion.3 = f32[816,2]{1,0:T(8,128)S(1)} fusion(f32[2,64,17]{0,1,2:T(8,128)S(1)} %bitcast.184, s32[816]{0:T(1024)S(1)} %reshape.192), kind=kCustom, calls=%fused_computation.3 | custom fusion | bytes 19584 | tf_op jit(solution)/shard_map/gather | solution.py:31
  266.5 91.0 %while.60 = (s32[]{:T(128)}, f32[]{:T(128)}, f32[640,640]{1,0:T(8,128)}, f32[640,640]{1,0:T(8,128)}, f32[640,4096]{1,0:T(8,128)}, /*index=5*/f32[4096]{0:T(1024)...) while((s32[]{:T(128)}, f32[]{:T(128)}, ...), condition=%wide.region_12.13_spmd.clone, body=%wide.region_7.12_spmd.clone.sunk | while | flops 8649718784 | bytes 146314000 | solution.py:183
  269.0 11.2 %fusion.89 = bf16[816,4096]{1,0:T(8,128)(2,1)} fusion(f32[2,816,4096]{2,1,0:T(8,128)} %get-tuple-element.1259, s32[]{:T(128)} %get-tuple-element.1229, f32[816]{0:T(1024)S(1)} %reshape.215, s32[816]{0:T(1024)S(1)} %eq.189, f32[816]{0:T(1024)S(1)} %exp.63, f32[816]{0:T(1024)S(1)} %add.404, pred[4096]{0:T(1024)(128)(4,1)S(1)} %iota_compare_fusion.4), kind=kLoop, calls=%fused_computation.33.clone.1 | loop fusion | flops 23396352 | bytes 20071172 | tf_op jit(solution)/shard_map/while/body/eval_jaxpr/convert_element_type | solution.py:134
  280.2 10.6 %select_add_fusion.12 = f32[640,4096]{1,0:T(8,128)} fusion(f32[640,4096]{1,0:T(8,128)} %get-tuple-element.1233, bf16[816,4096]{1,0:T(8,128)(2,1)} %fusion.89, pred[]{:T(512)S(6)} %compare.12, bf16[2,816,640]{2,1,0:T(8,128)(2,1)} %get-tuple-element.1266, s32[]{:T(128)} %get-tuple-element.1229), kind=kOutput, calls=%fused_computation.36.clone.1 | convolution fusion | flops 4283432960 | bytes 28701184 | tf_op jit(solution)/shard_map/while/body/eval_jaxpr/dot_general | solution.py:135
  290.8 8.1 %subtract_multiply_fusion.2 = f32[816,640]{1,0:T(8,128)} fusion(bf16[816,4096]{1,0:T(8,128)(2,1)S(1)} %copy-done, bf16[640,4096]{1,0:T(8,128)(2,1)S(1)} %bitcast.202, bf16[2,816,640]{2,1,0:T(8,128)(2,1)} %get-tuple-element.1266, s32[]{:T(128)} %get-tuple-element.1229), kind=kOutput, calls=%fused_computation.37.clone.1 | convolution fusion | flops 4280279040 | bytes 15060996 | tf_op jit(solution)/shard_map/while/body/eval_jaxpr/dot_general | solution.py:139
  312.2 11.2 %fusion.89 = bf16[816,4096]{1,0:T(8,128)(2,1)} fusion(f32[2,816,4096]{2,1,0:T(8,128)} %get-tuple-element.1259, s32[]{:T(128)} %get-tuple-element.1229, f32[816]{0:T(1024)S(1)} %reshape.215, s32[816]{0:T(1024)S(1)} %eq.189, f32[816]{0:T(1024)S(1)} %exp.63, f32[816]{0:T(1024)S(1)} %add.404, pred[4096]{0:T(1024)(128)(4,1)S(1)} %iota_compare_fusion.4), kind=kLoop, calls=%fused_computation.33.clone.1 | loop fusion | flops 23396352 | bytes 20071172 | tf_op jit(solution)/shard_map/while/body/eval_jaxpr/convert_element_type | solution.py:134
  323.4 12.1 %select_add_fusion.12 = f32[640,4096]{1,0:T(8,128)} fusion(f32[640,4096]{1,0:T(8,128)} %get-tuple-element.1233, bf16[816,4096]{1,0:T(8,128)(2,1)} %fusion.89, pred[]{:T(512)S(6)} %compare.12, bf16[2,816,640]{2,1,0:T(8,128)(2,1)} %get-tuple-element.1266, s32[]{:T(128)} %get-tuple-element.1229), kind=kOutput, calls=%fused_computation.36.clone.1 | convolution fusion | flops 4283432960 | bytes 28701184 | tf_op jit(solution)/shard_map/while/body/eval_jaxpr/dot_general | solution.py:135
  335.8 8.1 %subtract_multiply_fusion.2 = f32[816,640]{1,0:T(8,128)} fusion(bf16[816,4096]{1,0:T(8,128)(2,1)S(1)} %copy-done, bf16[640,4096]{1,0:T(8,128)(2,1)S(1)} %bitcast.202, bf16[2,816,640]{2,1,0:T(8,128)(2,1)} %get-tuple-element.1266, s32[]{:T(128)} %get-tuple-element.1229), kind=kOutput, calls=%fused_computation.37.clone.1 | convolution fusion | flops 4280279040 | bytes 15060996 | tf_op jit(solution)/shard_map/while/body/eval_jaxpr/dot_general | solution.py:139
  359.4 44.8 %all-reduce.5 = (f32[4096]{0:T(1024)S(1)}, f32[640]{0:T(1024)S(1)}, f32[]{:T(128)}, f32[]{:T(128)}) all-reduce(f32[4096]{0:T(1024)S(1)} %get-tuple-element.406, f32[640]{0:T(1024)S(1)} %get-tuple-element.407, f32[]{:T(128)} %get-tuple-element.408, f32[]{:T(128)S(6)} %convert_element_type.42), channel_id=1, replica_groups=mesh['dp'=8,'rep'=4] {'dp','rep'}, use_global_device_ids=true, to_apply=%region_19.20 | all-reduce | flops 4738 | bytes 37904 | tf_op jit(solution)/shard_map/psum | solution.py:205
  406.7 199.6 %all-reduce.9.cloned.1.call-done = (f32[640,640]{1,0:T(8,128)}, f32[640,640]{1,0:T(8,128)}, f32[640,4096]{1,0:T(8,128)}) async-done(((f32[640,640]{1,0:T(8,128)}, f32[640,640]{1,0:T(8,128)}, f32[640,4096]{1,0:T(8,128)}), (f32[640,640]{1,0:T(8,128)}, f32[640,640]{1,0:T(8,128)}, f32[640,4096]{1,0:T(8,128)})) %all-reduce.9.cloned.1.call-update) | async-done | bytes 13762576 | tf_op jit(solution)/shard_map/psum | solution.py:205
  606.3 7.4 %multiply_reduce_fusion = f32[]{:T(128)} fusion(f32[640,4096]{1,0:T(8,128)} %get-tuple-element.759), kind=kLoop, calls=%fused_computation.83 | loop fusion | flops 5242879 | bytes 10485764 | tf_op jit(solution)/shard_map/reduce_sum | solution.py:194
  619.2 9.7 %broadcast_multiply_fusion = f32[640,4096]{1,0:T(8,128)} fusion(f32[640,4096]{1,0:T(8,128)} %get-tuple-element.759, f32[]{:T(128)S(6)} %rsqrt.3), kind=kLoop, calls=%fused_computation.84 | loop fusion | flops 2621440 | bytes 20971524 | tf_op jit(solution)/shard_map/mul | solution.py:207
  (973 shorter events, 131.0 us)
Async XLA Ops:
  7.2 599.1 %all-reduce.9.cloned.1.call-start = ((), (), s32[]{:S(2)}) async-start(), calls=%async_computation | async-start | bytes 27525120 | tf_op jit(solution)/shard_map/psum | solution.py:205
  11.0 89.7 %copy-start.5 = (s32[64,17,1]{1,0,2:T(8,128)S(1)}, s32[64,17,1]{1,0,2:T(8,128)}, u32[]{:S(2)}) copy-start(s32[64,17,1]{1,0,2:T(8,128)} %fusion.34) | copy-start | bytes 13060
  11.0 115.0 %copy-start.14 = (pred[64,17]{1,0:T(8,128)(4,1)S(1)}, pred[64,17]{1,0:T(8,128)(4,1)}, u32[]{:S(2)}) copy-start(pred[64,17]{1,0:T(8,128)(4,1)} %compare_and_fusion) | copy-start | bytes 3268
  11.0 115.1 %copy-start.6 = (s32[64,17]{1,0:T(8,128)S(1)}, s32[64,17]{1,0:T(8,128)}, u32[]{:S(2)}) copy-start(s32[64,17]{1,0:T(8,128)} %iota_subtract_fusion) | copy-start | bytes 13060
  11.0 115.2 %copy-start.16 = (f32[17]{0:T(128)S(1)}, f32[17]{0:T(128)}, u32[]{:S(2)}) copy-start(f32[17]{0:T(128)} %compare_select_fusion.7) | copy-start | bytes 208
  11.1 115.2 %copy-start.7 = (s32[2]{0:T(128)S(1)}, s32[2]{0:T(128)}, u32[]{:S(2)}) copy-start(s32[2]{0:T(128)} %param.20) | copy-start | bytes 28
  11.1 115.2 %copy-start.10 = (f32[64,2,17]{2,1,0:T(2,128)S(1)}, f32[64,2,17]{2,1,0:T(2,128)}, u32[]{:S(2)}) copy-start(f32[64,2,17]{2,1,0:T(2,128)} %custom-call.20) | copy-start | bytes 26116
  11.1 115.2 %copy-start.11 = (f32[64,2,17]{2,1,0:T(2,128)S(1)}, f32[64,2,17]{2,1,0:T(2,128)}, u32[]{:S(2)}) copy-start(f32[64,2,17]{2,1,0:T(2,128)} %custom-call.21) | copy-start | bytes 26116
  11.1 115.2 %copy-start.12 = (f32[64,2,17]{2,1,0:T(2,128)S(1)}, f32[64,2,17]{2,1,0:T(2,128)}, u32[]{:S(2)}) copy-start(f32[64,2,17]{2,1,0:T(2,128)} %custom-call.22) | copy-start | bytes 26116
  11.1 115.2 %copy-start.13 = (s32[2]{0:T(128)S(1)}, s32[2]{0:T(128)}, u32[]{:S(2)}) copy-start(s32[2]{0:T(128)} %param.19) | copy-start | bytes 28
  11.1 115.2 %copy-start.15 = (f32[2,17]{1,0:T(2,128)S(1)}, f32[2,17]{1,0:T(2,128)}, u32[]{:S(2)}) copy-start(f32[2,17]{1,0:T(2,128)} %custom-call.10) | copy-start | bytes 412
  99.7 134.1 %copy-start.9 = (s32[48,17,1]{1,0,2:T(8,128)S(1)}, s32[48,17,1]{1,0,2:T(8,128)}, u32[]{:S(2)}) copy-start(s32[48,17,1]{1,0,2:T(8,128)} %fusion.37) | copy-start | bytes 9796
  113.2 153.3 %copy-start.4 = (bf16[2,48,640]{2,1,0:T(8,128)(2,1)S(1)}, bf16[2,48,640]{2,1,0:T(8,128)(2,1)}, u32[]{:S(2)}) copy-start(bf16[2,48,640]{2,1,0:T(8,128)(2,1)} %get-tuple-element.1284) | copy-start | bytes 368644
  113.2 153.3 %copy-start.18 = (s32[2,16]{1,0:T(2,128)S(1)}, s32[2,16]{1,0:T(2,128)}, u32[]{:S(2)}) copy-start(s32[2,16]{1,0:T(2,128)} %get-tuple-element.1288) | copy-start | bytes 388
  269.0 21.8 %slice-start.2 = ((s8[5242880]{0:T(1024)(128)(4,1)}), s8[1048576]{0:T(1024)(128)(4,1)S(1)}, s32[]{:S(2)}) async-start(s8[5242880]{0:T(1024)(128)(4,1)} %bitcast.201), calls=%async_computation.3 | async-start | bytes 2097152 | tf_op jit(solution)/shard_map/while
  280.2 10.6 %copy-start = (bf16[816,4096]{1,0:T(8,128)(2,1)S(1)}, bf16[816,4096]{1,0:T(8,128)(2,1)}, u32[]{:S(2)}) copy-start(bf16[816,4096]{1,0:T(8,128)(2,1)} %fusion.89) | copy-start | bytes 20054020 | tf_op jit(solution)/shard_map/while
  280.2 10.6 %slice-start.3 = ((s8[5242880]{0:T(1024)(128)(4,1)}), s8[4194304]{0:T(1024)(128)(4,1)S(1)}, s32[]{:S(2)}) async-start(s8[5242880]{0:T(1024)(128)(4,1)} %bitcast.201), calls=%async_computation.4 | async-start | bytes 8388608 | tf_op jit(solution)/shard_map/while
  299.0 8.8 %slice-start = ((s8[6684672]{0:T(1024)(128)(4,1)}), s8[2490368]{0:T(1024)(128)(4,1)S(1)}, s32[]{:S(2)}) async-start(s8[6684672]{0:T(1024)(128)(4,1)} %bitcast.181), calls=%async_computation.1 | async-start | bytes 4980736 | tf_op jit(solution)/shard_map/while
  312.2 23.3 %slice-start.2 = ((s8[5242880]{0:T(1024)(128)(4,1)}), s8[1048576]{0:T(1024)(128)(4,1)S(1)}, s32[]{:S(2)}) async-start(s8[5242880]{0:T(1024)(128)(4,1)} %bitcast.201), calls=%async_computation.3 | async-start | bytes 2097152 | tf_op jit(solution)/shard_map/while
  323.4 12.1 %copy-start = (bf16[816,4096]{1,0:T(8,128)(2,1)S(1)}, bf16[816,4096]{1,0:T(8,128)(2,1)}, u32[]{:S(2)}) copy-start(bf16[816,4096]{1,0:T(8,128)(2,1)} %fusion.89) | copy-start | bytes 20054020 | tf_op jit(solution)/shard_map/while
  323.4 12.4 %slice-start.3 = ((s8[5242880]{0:T(1024)(128)(4,1)}), s8[4194304]{0:T(1024)(128)(4,1)S(1)}, s32[]{:S(2)}) async-start(s8[5242880]{0:T(1024)(128)(4,1)} %bitcast.201), calls=%async_computation.4 | async-start | bytes 8388608 | tf_op jit(solution)/shard_map/while
  343.9 11.7 %slice-start = ((s8[6684672]{0:T(1024)(128)(4,1)}), s8[2490368]{0:T(1024)(128)(4,1)S(1)}, s32[]{:S(2)}) async-start(s8[6684672]{0:T(1024)(128)(4,1)} %bitcast.181), calls=%async_computation.1 | async-start | bytes 4980736 | tf_op jit(solution)/shard_map/while
  347.0 8.6 %slice-start.1 = ((s8[6684672]{0:T(1024)(128)(4,1)}), s8[4194304]{0:T(1024)(128)(4,1)S(1)}, s32[]{:S(2)}) async-start(s8[6684672]{0:T(1024)(128)(4,1)} %bitcast.181), calls=%async_computation.2 | async-start | bytes 8388608 | tf_op jit(solution)/shard_map/while
  606.3 7.4 %copy-start.3 = (f32[640,640]{1,0:T(8,128)S(1)}, f32[640,640]{1,0:T(8,128)}, u32[]{:S(2)}) copy-start(f32[640,640]{1,0:T(8,128)} %get-tuple-element.758) | copy-start | bytes 4915204
  (7 other events, 33.2 us)
Sparse Core Ops, SparseCore 0:
  357.6 248.6 all-reduce.8
where the time goes:
time: 649 us; the launch traced here: 640 us
  waiting for transfers between devices  200 us (31%)
  local copies, waits for them, and re-layouts  149 us (23%)
  other arithmetic  109 us (17%)
  matrix products  68.8 us (11%)
  loops' own time  47.9 us (7%)
  blocking collectives  44.8 us (7%)
  between operations  21.2 us (3%)
    psum x1, waiting for transfers between devices, per_device(): lax.psum((grads[0], grads[1], grads[2], grads[3], grads[4]), ('dp', 'rep'))  200 us
    another operation x1, loops' own time, lattice(): lax.scan(both_ways, (first_diag, neg_grid), inputs)  46.1 us
    psum x1, blocking collectives, per_device(): lax.psum((grads[0], grads[1], grads[2], grads[3], grads[4]), ('dp', 'rep'))  44.8 us
    dynamic_slice x256, local copies, waits for them, and re-layouts, lattice(): lax.scan(both_ways, (first_diag, neg_grid), inputs)  39.8 us
    gather x9, local copies, waits for them, and re-layouts, unskewed(): by_utterance[:, frame_ids[:, None] + positions[None, :], positions[None, :]]  30.5 us
    reduce_sum x2, other arithmetic, joint_forward(): jnp.sum(jnp.where(is_target, log_probs, 0.0), axis=1)  25.4 us
    gather x6, local copies, waits for them, and re-layouts, skewed(): grid[:, jnp.clip(frame_index, 0, num_frames - 1), positions[None, :]]  25.2 us
    dynamic_update_slice x6, local copies, waits for them, and re-layouts, local_sums(): lax.scan(forward_one, None, (enc, pred, labels))  24.7 us
  transfers between devices with their start and end apart: 1, of which 1 were waited for; matrix products, arithmetic and copies ran while one was open for 0% of the time, Pallas kernels for 0%

commit v1 on v0

--- a/solution.py
+++ b/solution.py
@@ -196,13 +196,18 @@
 
 
 def per_device(enc, pred, labels, frame_len, label_len, w_enc, w_pred, b_joint, w_out, b_out):
+
+    def vector_put(load):
+        wide_out = lax.psum(lax.psum(load, "dp"), "rep")
+        return wide_out
+
     loss_local, grads = local_sums(
         enc, pred, labels, frame_len, label_len, w_enc, w_pred, b_joint, w_out, b_out
     )
     count_local = jnp.sum(label_len).astype(jnp.float32)
     param_count = jnp.float32(w_enc.size + w_pred.size + w_out.size + b_out.size + b_joint.size)
     loss_total, label_total = lax.psum((loss_local, count_local), ("dp", "rep"))
-    summed = lax.psum((grads[0], grads[1], grads[2], grads[3], grads[4]), ("dp", "rep"))
+    summed = vector_put((grads[0], grads[1], grads[2], grads[3], grads[4]))
     scale = lax.rsqrt(squares(summed) / param_count + EPS)
     result = tuple((item * scale for item in summed))
     return (result[0], result[1], result[2], result[3], result[4], loss_total / label_total)

time: 649 us -> 1070 us (1.65)
  waiting for transfers between devices: 200 us -> 578 us
  blocking collectives: 44.8 us -> 90.4 us
    psum x1 -> x2, waiting for transfers between devices: 200 us -> 578 us  [vector_put(): wide_out = lax.psum(lax.psum(load, 'dp'), 'rep')]
    psum x1 -> x3, blocking collectives: 44.8 us -> 90.4 us  [the longest x2 49.2 us: vector_put(): wide_out = lax.psum(lax.psum(load, 'dp'), 'rep')]
  transfers between devices with their start and end apart: 1 -> 2, of which waited for: 1 -> 2; matrix products, arithmetic and copies ran while one was open for 0% -> 0% of each run, Pallas kernels for 0% -> 0%
where the time goes in v1:
time: 1070 us; the launch traced here: 1060 us
  waiting for transfers between devices  578 us (54%)
  local copies, waits for them, and re-layouts  149 us (14%)
  other arithmetic  109 us (10%)
  blocking collectives  90.4 us (8%)
  matrix products  68.8 us (6%)
  loops' own time  48.1 us (4%)
  between operations  21.3 us (2%)
    psum x2, waiting for transfers between devices, vector_put(): wide_out = lax.psum(lax.psum(load, 'dp'), 'rep')  578 us
    psum x2, blocking collectives, vector_put(): wide_out = lax.psum(lax.psum(load, 'dp'), 'rep')  49.2 us
    another operation x1, loops' own time, lattice(): lax.scan(both_ways, (first_diag, neg_grid), inputs)  46.1 us
    psum x1, blocking collectives, per_device(): loss_total, label_total = lax.psum((loss_local, count_local), ('dp', 'rep'))  41.2 us
    dynamic_slice x256, local copies, waits for them, and re-layouts, lattice(): lax.scan(both_ways, (first_diag, neg_grid), inputs)  39.8 us
    gather x9, local copies, waits for them, and re-layouts, unskewed(): by_utterance[:, frame_ids[:, None] + positions[None, :], positions[None, :]]  30.3 us
    reduce_sum x2, other arithmetic, joint_forward(): jnp.sum(jnp.where(is_target, log_probs, 0.0), axis=1)  25.4 us
    gather x6, local copies, waits for them, and re-layouts, skewed(): grid[:, jnp.clip(frame_index, 0, num_frames - 1), positions[None, :]]  25.2 us
  transfers between devices with their start and end apart: 2, of which 2 were waited for; matrix products, arithmetic and copies ran while one was open for 0% of the time, Pallas kernels for 0%

profile of v1, /device:TPU:0, one launch (start us, length us, event | category | flops | bytes accessed | tf_op | source)
XLA Modules:
  0.0 1064.1 jit_solution(16192252922041012584)
XLA Ops:
  11.1 88.6 %while.58 = (s32[]{:T(128)}, bf16[2,816,640]{2,1,0:T(8,128)(2,1)}, f32[2,816,4096]{2,1,0:T(8,128)}, f32[2,48,17]{2,1,0:T(8,128)S(1)}, f32[2,48,17]{2,1,0:T(8,128...) while((s32[]{:T(128)}, bf16[2,816,640]{2,1,0:T(8,128)(2,1)}, ...), condition=%wide.region_4.5_spmd, body=%wide.region_0.4_spmd.sunk | while | flops 4369261056 | bytes 147507888 | solution.py:167
  28.9 12.7 %select_reduce_fusion.2 = (f32[816]{0:T(1024)S(1)}, f32[816,4096]{1,0:T(8,128)}) fusion(s32[816]{0:T(1024)S(1)} %eq.178, f32[816]{0:T(1024)S(1)} %log.11, f32[816]{0:T(1024)S(1)} %get-tuple-element.1058, f32[816,4096]{1,0:T(8,128)} %copy-done.1, f32[4096]{0:T(1024)S(1)} %convert_element_type.65), kind=kLoop, calls=%fused_computation.62.clone.1 | loop fusion | flops 20053200 | bytes 26768128 | tf_op jit(solution)/shard_map/while/body/eval_jaxpr/reduce_sum | solution.py:110
  43.1 11.3 %bitcast_dynamic-update-slice_fusion.5 = f32[2,816,4096]{2,1,0:T(8,128)} fusion(f32[2,816,4096]{2,1,0:T(8,128)} %get-tuple-element.1125, s32[]{:T(128)} %get-tuple-element.1123, f32[816,4096]{1,0:T(8,128)} %get-tuple-element.1059), kind=kLoop, calls=%fused_computation.61.clone.1 | loop fusion | bytes 26739200 | tf_op jit(solution)/shard_map/while/body/jit(dynamic_update_index_in_dim)/dynamic_update_slice | solution.py:167
  73.2 12.7 %select_reduce_fusion.2 = (f32[816]{0:T(1024)S(1)}, f32[816,4096]{1,0:T(8,128)}) fusion(s32[816]{0:T(1024)S(1)} %eq.178, f32[816]{0:T(1024)S(1)} %log.11, f32[816]{0:T(1024)S(1)} %get-tuple-element.1058, f32[816,4096]{1,0:T(8,128)} %copy-done.1, f32[4096]{0:T(1024)S(1)} %convert_element_type.65), kind=kLoop, calls=%fused_computation.62.clone.1 | loop fusion | flops 20053200 | bytes 26768128 | tf_op jit(solution)/shard_map/while/body/eval_jaxpr/reduce_sum | solution.py:110
  87.3 11.3 %bitcast_dynamic-update-slice_fusion.5 = f32[2,816,4096]{2,1,0:T(8,128)} fusion(f32[2,816,4096]{2,1,0:T(8,128)} %get-tuple-element.1125, s32[]{:T(128)} %get-tuple-element.1123, f32[816,4096]{1,0:T(8,128)} %get-tuple-element.1059), kind=kLoop, calls=%fused_computation.61.clone.1 | loop fusion | bytes 26739200 | tf_op jit(solution)/shard_map/while/body/jit(dynamic_update_index_in_dim)/dynamic_update_slice | solution.py:167
  100.8 12.3 %gather_fusion = f32[1088,2]{1,0:T(8,128)S(1)} fusion(f32[2,48,17]{0,1,2:T(8,128)S(1)} %copy.55, s32[1088]{0:T(1024)S(1)} %reshape.180), kind=kCustom, calls=%fused_computation | custom fusion | bytes 26112 | tf_op jit(solution)/shard_map/gather | solution.py:21
  113.6 12.1 %gather_fusion.1 = f32[1088,2]{1,0:T(8,128)S(1)} fusion(f32[2,48,17]{0,1,2:T(8,128)S(1)} %copy.57, s32[1088]{0:T(1024)S(1)} %reshape.180), kind=kCustom, calls=%fused_computation.1 | custom fusion | bytes 26112 | tf_op jit(solution)/shard_map/gather | solution.py:21
  126.3 106.5 %while.59 = (s32[]{:T(128)}, f32[2,17]{1,0:T(2,128)S(1)}, f32[2,17]{1,0:T(2,128)S(1)}, f32[64,2,17]{2,1,0:T(2,128)S(1)}, f32[64,2,17]{2,1,0:T(2,128)S(1)}, /*ind...) while((s32[]{:T(128)}, f32[2,17]{1,0:T(2,128)S(1)}, ...), condition=%wide.region_6.7_spmd.clone, body=%wide.region_5.6_spmd.clone.sunk | while | flops 1434 | bytes 22799 | solution.py:84
  233.9 9.8 gather_fusion.2
  245.2 9.8 gather_fusion.4
  256.0 9.8 gather_fusion.3
  266.2 91.1 %while.60 = (s32[]{:T(128)}, f32[]{:T(128)}, f32[640,640]{1,0:T(8,128)}, f32[640,640]{1,0:T(8,128)}, f32[640,4096]{1,0:T(8,128)}, /*index=5*/f32[4096]{0:T(1024)...) while((s32[]{:T(128)}, f32[]{:T(128)}, ...), condition=%wide.region_12.13_spmd.clone, body=%wide.region_7.12_spmd.clone.sunk | while | flops 8649718784 | bytes 146314000 | solution.py:183
  269.0 11.2 %fusion.89 = bf16[816,4096]{1,0:T(8,128)(2,1)} fusion(f32[2,816,4096]{2,1,0:T(8,128)} %get-tuple-element.1264, s32[]{:T(128)} %get-tuple-element.1234, f32[816]{0:T(1024)S(1)} %reshape.215, s32[816]{0:T(1024)S(1)} %eq.189, f32[816]{0:T(1024)S(1)} %exp.63, f32[816]{0:T(1024)S(1)} %add.414, pred[4096]{0:T(1024)(128)(4,1)S(1)} %iota_compare_fusion.4), kind=kLoop, calls=%fused_computation.33.clone.1 | loop fusion | flops 23396352 | bytes 20071172 | tf_op jit(solution)/shard_map/while/body/eval_jaxpr/convert_element_type | solution.py:134
  280.2 10.6 select_add_fusion.12
  290.8 8.1 subtract_multiply_fusion.2
  312.2 11.2 %fusion.89 = bf16[816,4096]{1,0:T(8,128)(2,1)} fusion(f32[2,816,4096]{2,1,0:T(8,128)} %get-tuple-element.1264, s32[]{:T(128)} %get-tuple-element.1234, f32[816]{0:T(1024)S(1)} %reshape.215, s32[816]{0:T(1024)S(1)} %eq.189, f32[816]{0:T(1024)S(1)} %exp.63, f32[816]{0:T(1024)S(1)} %add.414, pred[4096]{0:T(1024)(128)(4,1)S(1)} %iota_compare_fusion.4), kind=kLoop, calls=%fused_computation.33.clone.1 | loop fusion | flops 23396352 | bytes 20071172 | tf_op jit(solution)/shard_map/while/body/eval_jaxpr/convert_element_type | solution.py:134
  323.4 12.1 %select_add_fusion.12 = f32[640,4096]{1,0:T(8,128)} fusion(f32[640,4096]{1,0:T(8,128)} %get-tuple-element.1238, bf16[816,4096]{1,0:T(8,128)(2,1)} %fusion.89, pred[]{:T(512)S(6)} %compare.12, bf16[2,816,640]{2,1,0:T(8,128)(2,1)} %get-tuple-element.1271, s32[]{:T(128)} %get-tuple-element.1234), kind=kOutput, calls=%fused_computation.36.clone.1 | convolution fusion | flops 4283432960 | bytes 28701184 | tf_op jit(solution)/shard_map/while/body/eval_jaxpr/dot_general | solution.py:135
  335.8 8.1 subtract_multiply_fusion.2
  357.5 429.8 %all-reduce.13.cloned.1.call-done = (f32[640,640]{1,0:T(8,128)}, f32[640,640]{1,0:T(8,128)}, f32[640,4096]{1,0:T(8,128)}) async-done(((f32[640,640]{1,0:T(8,128)}, f32[640,640]{1,0:T(8,128)}, f32[640,4096]{1,0:T(8,128)}), (f32[640,640]{1,0:T(8,128)}, f32[640,640]{1,0:T(8,128)}, f32[640,4096]{1,0:T(8,128)})) %all-reduce.13.cloned.1.call-update) | async-done | bytes 13762576 | tf_op jit(solution)/shard_map/psum | solution.py:201
  789.3 41.2 %all-reduce.5 = (f32[]{:T(128)}, f32[]{:T(128)}) all-reduce(f32[]{:T(128)} %get-tuple-element.408, f32[]{:T(128)S(6)} %convert_element_type.42), channel_id=1, replica_groups=mesh['dp'=8,'rep'=4] {'dp','rep'}, use_global_device_ids=true, to_apply=%region_28.29 | all-reduce | flops 2 | bytes 16 | tf_op jit(solution)/shard_map/psum | solution.py:209
  831.8 37.0 %all-reduce.6 = (f32[4096]{0:T(1024)S(1)}, f32[640]{0:T(1024)S(1)}) all-reduce(f32[4096]{0:T(1024)S(1)} %get-tuple-element.406, f32[640]{0:T(1024)S(1)} %get-tuple-element.407), channel_id=1, replica_groups=mesh['dp'=8,'rep'=4] {'dp'}, use_global_device_ids=true, to_apply=%region_22.23 | all-reduce | flops 4736 | bytes 37888 | tf_op jit(solution)/shard_map/psum | solution.py:201
  868.8 12.2 %all-reduce.8 = (f32[4096]{0:T(1024)S(1)}, f32[640]{0:T(1024)S(1)}) all-reduce(f32[4096]{0:T(1024)S(1)} %get-tuple-element.755, f32[640]{0:T(1024)S(1)} %get-tuple-element.756), channel_id=1, replica_groups=mesh['dp'=8,'rep'=4] {'rep'}, use_global_device_ids=true, to_apply=%region_23.24 | all-reduce | flops 4736 | bytes 37888 | tf_op jit(solution)/shard_map/psum | solution.py:201
  882.2 148.4 %all-reduce.15.cloned.1.call-done = (f32[640,640]{1,0:T(8,128)}, f32[640,640]{1,0:T(8,128)}, f32[640,4096]{1,0:T(8,128)}) async-done(((f32[640,640]{1,0:T(8,128)}, f32[640,640]{1,0:T(8,128)}, f32[640,4096]{1,0:T(8,128)}), (f32[640,640]{1,0:T(8,128)}, f32[640,640]{1,0:T(8,128)}, f32[640,4096]{1,0:T(8,128)})) %all-reduce.15.cloned.1.call-update) | async-done | bytes 13762576 | tf_op jit(solution)/shard_map/psum | solution.py:201
  1043.5 9.7 broadcast_multiply_fusion
  (978 shorter events, 153.4 us)
Async XLA Ops:
  7.2 780.1 %all-reduce.13.cloned.1.call-start = ((), (), s32[]{:S(2)}) async-start(), calls=%async_computation | async-start | bytes 27525120 | tf_op jit(solution)/shard_map/psum | solution.py:201
  11.0 89.7 %copy-start.5 = (s32[64,17,1]{1,0,2:T(8,128)S(1)}, s32[64,17,1]{1,0,2:T(8,128)}, u32[]{:S(2)}) copy-start(s32[64,17,1]{1,0,2:T(8,128)} %fusion.34) | copy-start | bytes 13060
  11.0 115.0 %copy-start.14 = (pred[64,17]{1,0:T(8,128)(4,1)S(1)}, pred[64,17]{1,0:T(8,128)(4,1)}, u32[]{:S(2)}) copy-start(pred[64,17]{1,0:T(8,128)(4,1)} %compare_and_fusion) | copy-start | bytes 3268
  11.0 115.1 %copy-start.6 = (s32[64,17]{1,0:T(8,128)S(1)}, s32[64,17]{1,0:T(8,128)}, u32[]{:S(2)}) copy-start(s32[64,17]{1,0:T(8,128)} %iota_subtract_fusion) | copy-start | bytes 13060
  11.0 115.2 %copy-start.16 = (f32[17]{0:T(128)S(1)}, f32[17]{0:T(128)}, u32[]{:S(2)}) copy-start(f32[17]{0:T(128)} %compare_select_fusion.7) | copy-start | bytes 208
  11.1 115.2 %copy-start.7 = (s32[2]{0:T(128)S(1)}, s32[2]{0:T(128)}, u32[]{:S(2)}) copy-start(s32[2]{0:T(128)} %param.20) | copy-start | bytes 28
  11.1 115.2 %copy-start.10 = (f32[64,2,17]{2,1,0:T(2,128)S(1)}, f32[64,2,17]{2,1,0:T(2,128)}, u32[]{:S(2)}) copy-start(f32[64,2,17]{2,1,0:T(2,128)} %custom-call.20) | copy-start | bytes 26116
  11.1 115.2 %copy-start.11 = (f32[64,2,17]{2,1,0:T(2,128)S(1)}, f32[64,2,17]{2,1,0:T(2,128)}, u32[]{:S(2)}) copy-start(f32[64,2,17]{2,1,0:T(2,128)} %custom-call.21) | copy-start | bytes 26116
  11.1 115.2 %copy-start.12 = (f32[64,2,17]{2,1,0:T(2,128)S(1)}, f32[64,2,17]{2,1,0:T(2,128)}, u32[]{:S(2)}) copy-start(f32[64,2,17]{2,1,0:T(2,128)} %custom-call.22) | copy-start | bytes 26116
  11.1 115.2 %copy-start.13 = (s32[2]{0:T(128)S(1)}, s32[2]{0:T(128)}, u32[]{:S(2)}) copy-start(s32[2]{0:T(128)} %param.19) | copy-start | bytes 28
  11.1 115.2 %copy-start.15 = (f32[2,17]{1,0:T(2,128)S(1)}, f32[2,17]{1,0:T(2,128)}, u32[]{:S(2)}) copy-start(f32[2,17]{1,0:T(2,128)} %custom-call.10) | copy-start | bytes 412
  99.7 134.1 %copy-start.9 = (s32[48,17,1]{1,0,2:T(8,128)S(1)}, s32[48,17,1]{1,0,2:T(8,128)}, u32[]{:S(2)}) copy-start(s32[48,17,1]{1,0,2:T(8,128)} %fusion.37) | copy-start | bytes 9796
  113.2 153.1 %copy-start.4 = (bf16[2,48,640]{2,1,0:T(8,128)(2,1)S(1)}, bf16[2,48,640]{2,1,0:T(8,128)(2,1)}, u32[]{:S(2)}) copy-start(bf16[2,48,640]{2,1,0:T(8,128)(2,1)} %get-tuple-element.1299) | copy-start | bytes 368644
  113.2 153.1 %copy-start.18 = (s32[2,16]{1,0:T(2,128)S(1)}, s32[2,16]{1,0:T(2,128)}, u32[]{:S(2)}) copy-start(s32[2,16]{1,0:T(2,128)} %get-tuple-element.1307) | copy-start | bytes 388
  269.0 21.8 %slice-start.2 = ((s8[5242880]{0:T(1024)(128)(4,1)}), s8[1048576]{0:T(1024)(128)(4,1)S(1)}, s32[]{:S(2)}) async-start(s8[5242880]{0:T(1024)(128)(4,1)} %bitcast.201), calls=%async_computation.4 | async-start | bytes 2097152 | tf_op jit(solution)/shard_map/while
  280.2 10.6 copy-start
  280.2 10.6 slice-start.3
  299.0 8.8 slice-start
  312.2 23.3 %slice-start.2 = ((s8[5242880]{0:T(1024)(128)(4,1)}), s8[1048576]{0:T(1024)(128)(4,1)S(1)}, s32[]{:S(2)}) async-start(s8[5242880]{0:T(1024)(128)(4,1)} %bitcast.201), calls=%async_computation.4 | async-start | bytes 2097152 | tf_op jit(solution)/shard_map/while
  323.4 12.1 %copy-start = (bf16[816,4096]{1,0:T(8,128)(2,1)S(1)}, bf16[816,4096]{1,0:T(8,128)(2,1)}, u32[]{:S(2)}) copy-start(bf16[816,4096]{1,0:T(8,128)(2,1)} %fusion.89) | copy-start | bytes 20054020 | tf_op jit(solution)/shard_map/while
  323.4 12.4 %slice-start.3 = ((s8[5242880]{0:T(1024)(128)(4,1)}), s8[4194304]{0:T(1024)(128)(4,1)S(1)}, s32[]{:S(2)}) async-start(s8[5242880]{0:T(1024)(128)(4,1)} %bitcast.201), calls=%async_computation.5 | async-start | bytes 8388608 | tf_op jit(solution)/shard_map/while
  343.9 11.7 %slice-start = ((s8[6684672]{0:T(1024)(128)(4,1)}), s8[2490368]{0:T(1024)(128)(4,1)S(1)}, s32[]{:S(2)}) async-start(s8[6684672]{0:T(1024)(128)(4,1)} %bitcast.181), calls=%async_computation.2 | async-start | bytes 4980736 | tf_op jit(solution)/shard_map/while
  347.0 8.6 slice-start.1
  357.4 673.1 %all-reduce.15.cloned.1.call-start = ((), (), s32[]{:S(2)}) async-start(), calls=%async_computation.1 | async-start | bytes 27525120 | tf_op jit(solution)/shard_map/psum | solution.py:201
  (8 other events, 40.6 us)
Sparse Core Ops, SparseCore 0:
  357.5 429.7 all-reduce.12
  790.0 240.4 all-reduce.14
